TPU v7x, 32 devices: a whole 2x2x4 slice. The times are simulated.
32 devices in a mesh: dp: 4 (over y, x), fsdp: 8 (over z, core).
Axes of the slice: x: 2, y: 2, z: 4, core: 2. Of those that a mesh axis runs over, the one named last changes fastest.
Arguments:
- tokens: bfloat16 [32768, 768], P(('dp', 'fsdp')), may hold values from -11 to 11
- attention: bfloat16 [768, 3072], P(None, 'fsdp'), may hold values from -2 to 2
- attvector: bfloat16 [3840], P('fsdp'), may hold values from -2 to 2
- expand: bfloat16 [768, 3072], P(None, 'fsdp'), may hold values from -0.21875 to 0.21875
- contract: bfloat16 [3072, 768], P('fsdp'), may hold values from -0.109375 to 0.109375
- feedvector: bfloat16 [5376], P('fsdp'), may hold values from -2 to 2
- lengths: int32 [64], P(('dp', 'fsdp')), may hold values from 1 to 512, 19660 in all
- cotangent: bfloat16 [32768, 768], P(('dp', 'fsdp')), may hold values from -6 to 6
Outputs:
- layer_output: bfloat16 [32768, 768], P(('dp', 'fsdp'))
- input_grad: bfloat16 [32768, 768], P(('dp', 'fsdp'))
- attention_grad: float32 [768, 3072], P(None, 'fsdp')
- attvector_grad: float32 [3840], P('fsdp')
- expand_grad: float32 [768, 3072], P(None, 'fsdp')
- contract_grad: float32 [3072, 768], P('fsdp')
- feedvector_grad: float32 [5376], P('fsdp')
- root_squares: float32 [3], replicated
Inputs may be any that keep to these rules, and one draw needn't show every extreme that they name: `lengths`: some row is full.
All inputs are finite; a program needn't handle non-finite values. No bound on the sum of `lengths` on one device may be relied on, other than what follows from the above.
Results may differ from a plain program's by a relative error of at most 0.015.
Values may be sent and summed in bfloat16 or wider, within the bound.
No kernel may reach another device: no remote copies, remote signals or barrier semaphores. Data moves between devices by JAX's collectives and lax.ppermute only.
A program may use at most 192 MiB of HBM per device.

v0:
```python
import math
import jax
import jax.numpy as jnp
from jax import lax
from jax.sharding import PartitionSpec as P

HEAD_DIM = 64
FF = 3072
EPSILON = 1e-12
NEGATIVE = -1000000000.0


def norm_forward(residual, scale_gain, shift_bias):
    centered = residual - jnp.mean(residual, axis=-1, keepdims=True)
    inverse = lax.rsqrt(jnp.mean(centered * centered, axis=-1, keepdims=True) + EPSILON)
    normed = centered * inverse
    return (normed * scale_gain + shift_bias, normed, inverse)


def norm_backward(upstream, normed, inverse, scale_gain):
    gain_grad = jnp.sum(upstream * normed, axis=0)
    shift_grad = jnp.sum(upstream, axis=0)
    scaled = upstream * scale_gain
    mean_plain = jnp.mean(scaled, axis=-1, keepdims=True)
    mean_normed = jnp.mean(scaled * normed, axis=-1, keepdims=True)
    return (inverse * (scaled - mean_plain - normed * mean_normed), gain_grad, shift_grad)


def masked_scores(queries, key_rows, live_mask):
    scale_factor = 1.0 / math.sqrt(queries.shape[-1])
    scores = (
        jnp.einsum("qhd,khd->hqk", queries, key_rows, preferred_element_type=jnp.float32)
        * scale_factor
    )
    return jnp.where(live_mask[None, None, :], scores, NEGATIVE)


def attend(block_item):
    queries, key_rows, value_rows, live_mask = block_item
    scores = masked_scores(queries, key_rows, live_mask)
    peak_score = jnp.max(scores, axis=-1, keepdims=True)
    totals = jnp.sum(jnp.exp(scores - peak_score), axis=-1, keepdims=True)
    logsum = peak_score + jnp.log(totals)
    softmax_low = jnp.exp(scores - logsum).astype(jnp.bfloat16)
    context = jnp.einsum(
        "hqk,khd->qhd", softmax_low, value_rows, preferred_element_type=jnp.float32
    )
    return (context.astype(jnp.bfloat16), logsum[..., 0])


def attend_back(block_item):
    queries, key_rows, value_rows, live_mask, logsum, context_grad = block_item
    scale_factor = 1.0 / math.sqrt(queries.shape[-1])
    scores = masked_scores(queries, key_rows, live_mask)
    softmax_wide = jnp.exp(scores - logsum[..., None])
    softmax_low = softmax_wide.astype(jnp.bfloat16)
    value_grad = jnp.einsum(
        "hqk,qhd->khd", softmax_low, context_grad, preferred_element_type=jnp.float32
    )
    weight_grad = jnp.einsum(
        "qhd,khd->hqk", context_grad, value_rows, preferred_element_type=jnp.float32
    )
    row_total = jnp.sum(softmax_wide * weight_grad, axis=-1, keepdims=True)
    score_grad = (softmax_wide * (weight_grad - row_total)).astype(jnp.bfloat16)
    query_grad = (
        jnp.einsum("hqk,khd->qhd", score_grad, key_rows, preferred_element_type=jnp.float32)
        * scale_factor
    )
    key_grad = (
        jnp.einsum("hqk,qhd->khd", score_grad, queries, preferred_element_type=jnp.float32)
        * scale_factor
    )
    return (
        query_grad.astype(jnp.bfloat16),
        key_grad.astype(jnp.bfloat16),
        value_grad.astype(jnp.bfloat16),
    )


def gelu_slope(inner_act):
    cumulative = 0.5 * (1.0 + lax.erf(inner_act * (1.0 / math.sqrt(2.0))))
    density = jnp.exp(-0.5 * inner_act * inner_act) * (1.0 / math.sqrt(2.0 * math.pi))
    return cumulative + inner_act * density


def column_sum(values):
    return jnp.sum(values, axis=0, dtype=jnp.float32)


def per_device(tokens, attention, attvector, expand, contract, feedvector, lengths, cotangent):
    model_width = tokens.shape[1]
    row_count = lengths.shape[0]
    positions = tokens.shape[0] // row_count
    head_count = model_width // HEAD_DIM
    attn_whole, attvec_whole = (
        lax.all_gather(attention, "fsdp", axis=1, tiled=True),
        lax.all_gather(attvector, "fsdp", axis=0, tiled=True),
    )
    expand_whole, contract_whole, feedvec_whole = (
        lax.all_gather(expand, "fsdp", axis=1, tiled=True),
        lax.all_gather(contract, "fsdp", axis=0, tiled=True),
        lax.all_gather(feedvector, "fsdp", axis=0, tiled=True),
    )
    attvec_wide = attvec_whole.astype(jnp.float32)
    feedvec_wide = feedvec_whole.astype(jnp.float32)
    query_bias = attvec_wide[:model_width]
    value_bias = attvec_wide[model_width : 2 * model_width]
    output_bias = attvec_wide[2 * model_width : 3 * model_width]
    first_gain = attvec_wide[3 * model_width : 4 * model_width]
    first_shift = attvec_wide[4 * model_width :]
    inner_bias = feedvec_wide[:FF]
    outer_bias = feedvec_wide[FF : FF + model_width]
    second_gain = feedvec_wide[FF + model_width : FF + 2 * model_width]
    second_shift = feedvec_wide[FF + 2 * model_width :]
    tokens_wide = tokens.astype(jnp.float32)
    projected = jnp.dot(
        tokens, attn_whole[:, : 3 * model_width], preferred_element_type=jnp.float32
    )
    queries = (projected[:, :model_width] + query_bias).astype(jnp.bfloat16)
    key_rows = projected[:, model_width : 2 * model_width].astype(jnp.bfloat16)
    value_rows = (projected[:, 2 * model_width :] + value_bias).astype(jnp.bfloat16)
    shape_four = (row_count, positions, head_count, HEAD_DIM)
    live_mask = jnp.arange(positions, dtype=jnp.int32)[None, :] < lengths[:, None]
    query_four = queries.reshape(shape_four)
    key_four = key_rows.reshape(shape_four)
    value_four = value_rows.reshape(shape_four)
    context, logsum = lax.map(attend, (query_four, key_four, value_four, live_mask))
    context_flat = context.reshape(-1, model_width)
    branch_attn = (
        jnp.dot(context_flat, attn_whole[:, 3 * model_width :], preferred_element_type=jnp.float32)
        + output_bias
    )
    hidden, normed_one, inverse_one = norm_forward(
        tokens_wide + branch_attn, first_gain, first_shift
    )
    hidden_low = hidden.astype(jnp.bfloat16)
    inner_act = jnp.dot(hidden_low, expand_whole, preferred_element_type=jnp.float32) + inner_bias
    gelu_low = jax.nn.gelu(inner_act, approximate=False).astype(jnp.bfloat16)
    branch_feed = jnp.dot(gelu_low, contract_whole, preferred_element_type=jnp.float32) + outer_bias
    result, normed_two, inverse_two = norm_forward(hidden + branch_feed, second_gain, second_shift)
    live_column = live_mask.reshape(-1, 1).astype(jnp.float32)
    squares = jnp.stack(
        [
            jnp.sum(live_column * tokens_wide * tokens_wide),
            jnp.sum(live_column * branch_attn * branch_attn),
            jnp.sum(live_column * branch_feed * branch_feed),
        ]
    )
    count_sum = jnp.sum(lengths).astype(jnp.float32)
    square_sums, count_total = lax.psum((squares, count_sum), ("dp", "fsdp"))
    root_squares = jnp.sqrt(square_sums / (count_total * model_width))
    back_attention, back_attvec = (
        lax.all_gather(attention, "fsdp", axis=1, tiled=True),
        lax.all_gather(attvector, "fsdp", axis=0, tiled=True),
    )
    back_expand, back_contract, back_feedvec = (
        lax.all_gather(expand, "fsdp", axis=1, tiled=True),
        lax.all_gather(contract, "fsdp", axis=0, tiled=True),
        lax.all_gather(feedvector, "fsdp", axis=0, tiled=True),
    )
    first_gain_back = back_attvec[3 * model_width : 4 * model_width].astype(jnp.float32)
    second_gain_back = back_feedvec[FF + model_width : FF + 2 * model_width].astype(jnp.float32)
    grad_two, second_gain_grad, second_shift_grad = norm_backward(
        cotangent.astype(jnp.float32), normed_two, inverse_two, second_gain_back
    )
    feed_out_grad = grad_two.astype(jnp.bfloat16)
    outer_bias_grad = column_sum(feed_out_grad)
    contract_grad = jnp.einsum(
        "nf,nd->fd", gelu_low, feed_out_grad, preferred_element_type=jnp.float32
    )
    gelu_grad = jnp.einsum(
        "nd,fd->nf", feed_out_grad, back_contract, preferred_element_type=jnp.float32
    )
    inner_grad = (gelu_grad * gelu_slope(inner_act)).astype(jnp.bfloat16)
    inner_bias_grad = column_sum(inner_grad)
    expand_grad = jnp.einsum(
        "nd,nf->df", hidden_low, inner_grad, preferred_element_type=jnp.float32
    )
    feedvec_grad = jnp.concatenate(
        [inner_bias_grad, outer_bias_grad, second_gain_grad, second_shift_grad]
    )
    feed_shards = (
        lax.psum_scatter(expand_grad, "fsdp", scatter_dimension=1, tiled=True),
        lax.psum_scatter(contract_grad, "fsdp", scatter_dimension=0, tiled=True),
        lax.psum_scatter(feedvec_grad, "fsdp", scatter_dimension=0, tiled=True),
    )
    hidden_grad = grad_two + jnp.einsum(
        "nf,df->nd", inner_grad, back_expand, preferred_element_type=jnp.float32
    )
    grad_one, first_gain_grad, first_shift_grad = norm_backward(
        hidden_grad, normed_one, inverse_one, first_gain_back
    )
    attn_out_grad = grad_one.astype(jnp.bfloat16)
    output_bias_grad = column_sum(attn_out_grad)
    output_weight_grad = jnp.einsum(
        "nd,ne->de", context_flat, attn_out_grad, preferred_element_type=jnp.float32
    )
    context_grad = jnp.einsum(
        "ne,de->nd",
        attn_out_grad,
        back_attention[:, 3 * model_width :],
        preferred_element_type=jnp.float32,
    ).astype(jnp.bfloat16)
    query_grad, key_grad, value_grad = lax.map(
        attend_back,
        (query_four, key_four, value_four, live_mask, logsum, context_grad.reshape(shape_four)),
    )
    projected_grad = jnp.concatenate(
        [
            query_grad.reshape(-1, model_width),
            key_grad.reshape(-1, model_width),
            value_grad.reshape(-1, model_width),
        ],
        axis=1,
    )
    query_bias_grad = column_sum(projected_grad[:, :model_width])
    value_bias_grad = column_sum(projected_grad[:, 2 * model_width :])
    projection_grad = jnp.einsum(
        "nd,ne->de", tokens, projected_grad, preferred_element_type=jnp.float32
    )
    input_grad = grad_one + jnp.einsum(
        "ne,de->nd",
        projected_grad,
        back_attention[:, : 3 * model_width],
        preferred_element_type=jnp.float32,
    )
    attention_grad = jnp.concatenate([projection_grad, output_weight_grad], axis=1)
    attvec_grad = jnp.concatenate(
        [query_bias_grad, value_bias_grad, output_bias_grad, first_gain_grad, first_shift_grad]
    )
    attn_shards = (
        lax.psum_scatter(attention_grad, "fsdp", scatter_dimension=1, tiled=True),
        lax.psum_scatter(attvec_grad, "fsdp", scatter_dimension=0, tiled=True),
    )
    finished = (
        lax.psum(attn_shards[0].astype(jnp.bfloat16), "dp").astype(jnp.float32),
        lax.psum(attn_shards[1].astype(jnp.bfloat16), "dp").astype(jnp.float32),
        lax.psum(feed_shards[0].astype(jnp.bfloat16), "dp").astype(jnp.float32),
        lax.psum(feed_shards[1].astype(jnp.bfloat16), "dp").astype(jnp.float32),
        lax.psum(feed_shards[2].astype(jnp.bfloat16), "dp").astype(jnp.float32),
    )
    return (
        result.astype(jnp.bfloat16),
        input_grad.astype(jnp.bfloat16),
        finished[0],
        finished[1],
        finished[2],
        finished[3],
        finished[4],
        root_squares,
    )


def solution(mesh):
    return jax.shard_map(
        per_device,
        mesh=mesh,
        in_specs=(
            P(("dp", "fsdp"), None),
            P(None, "fsdp"),
            P("fsdp"),
            P(None, "fsdp"),
            P("fsdp", None),
            P("fsdp"),
            P(("dp", "fsdp")),
            P(("dp", "fsdp"), None),
        ),
        out_specs=(
            P(("dp", "fsdp"), None),
            P(("dp", "fsdp"), None),
            P(None, "fsdp"),
            P("fsdp"),
            P(None, "fsdp"),
            P("fsdp", None),
            P("fsdp"),
            P(),
        ),
        check_vma=False,
    )
```

profile of v0, /device:TPU:0, one launch (start us, length us, event | category | flops | bytes accessed | tf_op | source)
XLA Modules:
  0.0 590.4 jit_solution(3069860904495769675)
XLA Ops:
  13.8 32.2 %all-reduce.6 = (bf16[3840]{0:T(1024)(128)(2,1)S(1)}, bf16[5376]{0:T(1024)(128)(2,1)S(1)}) all-reduce(bf16[3840]{0:T(1024)(128)(2,1)S(1)} %dynamic-update-slice, bf16[5376]{0:T(1024)(128)(2,1)S(1)} %dynamic-update-slice.1), channel_id=1, replica_groups=mesh['dp'=4,'fsdp'=8] {'fsdp'}, use_global_device_ids=true, to_apply=%add | all-reduce | flops 9216 | bytes 36864
  52.8 11.5 %all-gather.4.cloned.1.call-done = bf16[768,3072]{1,0:T(8,128)(2,1)} async-done(((bf16[768,384]{1,0:T(8,128)(2,1)}), bf16[768,3072]{1,0:T(8,128)(2,1)}) %all-gather.4.cloned.1.call-update) | async-done | bytes 4718608 | tf_op jit(solution)/shard_map/all_gather | solution.py:96
  64.3 5.8 fusion.87
  96.6 19.2 %while.26 = (s32[]{:T(128)}, bf16[2,512,12,64]{1,3,2,0:T(8,128)(2,1)}, f32[2,12,512]{2,1,0:T(8,128)S(1)}, bf16[2,512,12,64]{1,3,2,0:T(8,128)(2,1)}, pred[2,512]{...) while((s32[]{:T(128)}, ...), condition=%wide.region_3.4_spmd, body=%wide.region_0.3_spmd.sunk | while | flops 840296448 | bytes 47428224 | solution.py:127
  126.1 38.3 %fusion.59 = (bf16[1024,3072]{1,0:T(8,128)(2,1)}, f32[1024,3072]{1,0:T(8,128)}) fusion(f32[3072]{0:T(1024)S(1)} %slice.77, bf16[768,3072]{1,0:T(8,128)(2,1)} %all-gather.6.cloned.1.call-done, f32[1024,768]{0,1:T(8,128)S(1)} %get-tuple-element.245, f32[768]{0:T(1024)S(1)} %get-tuple-element.259, f32[768]{0:T(1024)S(1)} %get-tuple-element.258, ...), kind=kOutput, calls=%fused_computation.67 | convolution fusion | flops 5043388416 | bytes 26765312 | tf_op jit(solution)/shard_map/dot_general | solution.py:137
  167.6 12.3 %fusion.80 = (f32[]{:T(128)}, f32[]{:T(128)}, f32[]{:T(128)}, f32[1024]{0:T(1024)S(1)}, f32[1024,768]{0,1:T(8,128)S(1)}) fusion(bf16[1024,768]{0,1:T(8,128)(2,1)} %copy.66, f32[1024]{0:T(1024)S(1)} %bitcast.165, f32[1024,768]{0,1:T(8,128)} %get-tuple-element.267, f32[768]{0:T(1024)S(1)} %get-tuple-element.260, f32[768]{0:T(1024)S(1)} %copy-done.46, ...), kind=kOutput, calls=%fused_computation.106 | convolution fusion | flops 4845992960 | bytes 22048780 | tf_op jit(solution)/shard_map/dot_general | solution.py:139
  186.5 12.3 %convert_reduce_fusion = (f32[3072]{0:T(1024)}, bf16[1024,3072]{1,0:T(8,128)(2,1)S(1)}) fusion(f32[1024,3072]{1,0:T(8,128)S(1)} %copy-done.49, f32[3072]{0:T(1024)S(1)} %slice.77, bf16[1024,768]{0,1:T(8,128)(2,1)S(1)} %get-tuple-element.239, bf16[3072,768]{1,0:T(8,128)(2,1)S(1)} %bitcast.167), kind=kOutput, calls=%fused_computation.74 | convolution fusion | flops 4872729600 | bytes 25190400 | tf_op jit(solution)/shard_map/nd,fd->nf/dot_general | solution.py:171
  201.4 7.8 %fusion.99 = f32[768,3072]{1,0:T(8,128)} fusion(bf16[1024,3072]{1,0:T(8,128)(2,1)S(1)} %get-tuple-element.272, f32[1024,768]{0,1:T(8,128)S(1)} %copy-done.15, f32[768]{0:T(1024)S(1)} %get-tuple-element.259, f32[768]{0:T(1024)S(1)} %get-tuple-element.258, f32[1024]{0:T(1024)S(1)} %add_rsqrt_fusion.1, f32[1024]{0:T(1024)S(1)} %broadcast_multiply_fusion.5), kind=kOutput, calls=%fused_computation.169 | convolution fusion | flops 4835770368 | bytes 18888704 | tf_op jit(solution)/shard_map/nd,nf->df/dot_general | solution.py:176
  209.9 12.5 %multiply_reduce_fusion.1 = (f32[768]{0:T(1024)}, f32[1024]{0:T(1024)S(1)}, f32[1024]{0:T(1024)S(1)}, f32[768]{0:T(1024)}, f32[1024,768]{0,1:T(8,128)S(1)}) fusion(f32[1024,768]{0,1:T(8,128)} %copy-done.14, f32[1024]{0:T(1024)S(1)} %add_rsqrt_fusion.1, f32[1024]{0:T(1024)S(1)} %broadcast_multiply_fusion.5, f32[768]{0:T(1024)S(1)} %copy-done.36, ...), kind=kOutput, calls=%fused_computation.115 | convolution fusion | flops 4845989888 | bytes 22065152 | tf_op jit(solution)/shard_map/nf,df->nd/dot_general | solution.py:187
  235.9 48.7 %while.27 = (s32[]{:T(128)}, bf16[2,512,12,64]{1,3,2,0:T(8,128)(2,1)}, bf16[2,512,12,64]{1,3,2,0:T(8,128)(2,1)}, bf16[2,512,12,64]{1,3,2,0:T(8,128)(2,1)}, bf16[...) while((s32[]{:T(128)}, ...), condition=%wide.region_14.15_spmd, body=%wide.region_12.14_spmd.sunk | while | flops 2062411776 | bytes 152764272 | solution.py:204
  241.2 7.4 %multiply_reduce_fusion.7 = (f32[12,512]{1,0:T(8,128)S(1)}, f32[12,512,512]{1,2,0:T(8,128)}) fusion(f32[12,512,512]{1,2,0:T(8,128)S(1)} %fusion.154, f32[12,512]{1,0:T(8,128)S(1)} %dynamic-slice_bitcast_fusion.2, pred[512]{0:T(512)(128)(4,1)S(1)} %dynamic-slice_reduce_fusion.5, bf16[2,512,12,64]{1,3,2,0:T(8,128)(2,1)S(1)} %copy-done.5, ...), kind=kOutput, calls=%fused_computation.24.clone.1 | convolution fusion | flops 418375680 | bytes 26797568 | tf_op jit(solution)/shard_map/while/body/eval_jaxpr/qhd,khd->hqk/dot_general | solution.py:60
  248.5 7.3 %multiply_convert_fusion.4 = bf16[12,512,512]{1,2,0:T(8,128)(2,1)S(1)} fusion(f32[12,512,512]{1,2,0:T(8,128)} %get-tuple-element.389, f32[12,512,512]{1,2,0:T(8,128)S(1)} %fusion.154, f32[12,512]{1,0:T(8,128)S(1)} %get-tuple-element.390, f32[12,512]{1,0:T(8,128)S(1)} %dynamic-slice_bitcast_fusion.2, pred[512]{0:T(512)(128)(4,1)S(1)} %dynamic-slice_reduce_fusion.5), kind=kLoop, calls=%fused_computation.23.clone.1 | loop fusion | flops 18874368 | bytes 31506944 | tf_op jit(solution)/shard_map/while/body/eval_jaxpr/convert_element_type | solution.py:64
  265.3 7.4 %multiply_reduce_fusion.7 = (f32[12,512]{1,0:T(8,128)S(1)}, f32[12,512,512]{1,2,0:T(8,128)}) fusion(f32[12,512,512]{1,2,0:T(8,128)S(1)} %fusion.154, f32[12,512]{1,0:T(8,128)S(1)} %dynamic-slice_bitcast_fusion.2, pred[512]{0:T(512)(128)(4,1)S(1)} %dynamic-slice_reduce_fusion.5, bf16[2,512,12,64]{1,3,2,0:T(8,128)(2,1)S(1)} %copy-done.5, ...), kind=kOutput, calls=%fused_computation.24.clone.1 | convolution fusion | flops 418375680 | bytes 26797568 | tf_op jit(solution)/shard_map/while/body/eval_jaxpr/qhd,khd->hqk/dot_general | solution.py:60
  272.6 7.2 %multiply_convert_fusion.4 = bf16[12,512,512]{1,2,0:T(8,128)(2,1)S(1)} fusion(f32[12,512,512]{1,2,0:T(8,128)} %get-tuple-element.389, f32[12,512,512]{1,2,0:T(8,128)S(1)} %fusion.154, f32[12,512]{1,0:T(8,128)S(1)} %get-tuple-element.390, f32[12,512]{1,0:T(8,128)S(1)} %dynamic-slice_bitcast_fusion.2, pred[512]{0:T(512)(128)(4,1)S(1)} %dynamic-slice_reduce_fusion.5), kind=kLoop, calls=%fused_computation.23.clone.1 | loop fusion | flops 18874368 | bytes 31506944 | tf_op jit(solution)/shard_map/while/body/eval_jaxpr/convert_element_type | solution.py:64
  297.8 5.8 convolution_bitcast_fusion
  303.6 8.0 %pad_maximum_fusion = f32[768,3072]{0,1:T(8,128)} fusion(f32[768,768]{0,1:T(8,128)} %fusion.96, f32[768,2304]{0,1:T(8,128)} %convolution_bitcast_fusion), kind=kLoop, calls=%fused_computation.90 | loop fusion | flops 2359296 | bytes 18874368 | tf_op jit(solution)/shard_map/concatenate | solution.py:227
  311.7 10.0 %fusion.109 = f32[3072,768]{1,0:T(8,128)} fusion(bf16[1024,3072]{1,0:T(8,128)(2,1)} %get-tuple-element.268, bf16[1024,768]{0,1:T(8,128)(2,1)} %copy-done.27), kind=kOutput, calls=%fused_computation.176 | convolution fusion | flops 4831838208 | bytes 17301504 | tf_op jit(solution)/shard_map/nf,nd->fd/dot_general | solution.py:168
  326.9 40.2 %all-reduce.4 = (f32[3]{0:T(128)S(1)}, f32[]{:T(128)}) all-reduce(f32[3]{0:T(128)S(1)} %pad_maximum_fusion.2, f32[]{:T(128)S(6)} %convert_element_type.176), channel_id=1, replica_groups=mesh['dp'=4,'fsdp'=8] {'dp','fsdp'}, use_global_device_ids=true, to_apply=%region_37.38 | all-reduce | flops 4 | bytes 32 | tf_op jit(solution)/shard_map/psum | solution.py:150
  370.1 40.7 %reduce-scatter.4.cloned.1.call-done = f32[768,384]{0,1:T(8,128)} async-done(((f32[768,3072]{0,1:T(8,128)}), f32[768,384]{0,1:T(8,128)}) %reduce-scatter.4.cloned.1.call-update) | async-done | bytes 1179664 | tf_op jit(solution)/shard_map/reduce_scatter | solution.py:232
  412.9 97.9 %reduce-scatter.8.cloned.1.call-done = f32[384,768]{1,0:T(8,128)} async-done(((f32[3072,768]{1,0:T(8,128)}), f32[384,768]{1,0:T(8,128)}) %reduce-scatter.8.cloned.1.call-update) | async-done | bytes 1179664 | tf_op jit(solution)/shard_map/reduce_scatter | solution.py:184
  513.2 26.4 %all-reduce.5 = (bf16[3840]{0:T(1024)(128)(2,1)S(1)}, bf16[5376]{0:T(1024)(128)(2,1)S(1)}) all-reduce(f32[3840]{0:T(1024)S(1)} %constant_dynamic-update-slice_fusion.6, f32[5376]{0:T(1024)S(1)} %pad_maximum_fusion.1), channel_id=3, replica_groups=mesh['dp'=4,'fsdp'=8] {'fsdp'}, use_global_device_ids=true, to_apply=%region_22.23.clone | all-reduce | flops 9216 | bytes 55296
  539.7 9.9 %all-reduce.7 = (bf16[480]{0:T(512)(128)(2,1)S(1)}, bf16[672]{0:T(1024)(128)(2,1)S(1)}) all-reduce(bf16[480]{0:T(512)(128)(2,1)S(1)} %dynamic-slice.9, bf16[672]{0:T(1024)(128)(2,1)S(1)} %dynamic-slice.8), channel_id=1, replica_groups=mesh['dp'=4,'fsdp'=8] {'dp'}, use_global_device_ids=true, to_apply=%region_23.24 | all-reduce | flops 1152 | bytes 4608 | tf_op jit(solution)/shard_map/psum | solution.py:237
  552.4 8.3 %add_convert_fusion = bf16[1024,768]{0,1:T(8,128)(2,1)S(1)} fusion(f32[1024,768]{0,1:T(8,128)} %copy-done.20, bf16[1024,2304]{0,1:T(8,128)(2,1)} %copy-done.29, bf16[768,3072]{1,0:T(8,128)(2,1)} %all-gather.4.cloned.1.call-done), kind=kOutput, calls=%fused_computation.119 | convolution fusion | flops 3625451520 | bytes 12976128 | tf_op jit(solution)/shard_map/ne,de->nd/dot_general | solution.py:221
  563.4 14.3 %all-reduce.11.cloned.1.call-done = (bf16[768,384]{0,1:T(8,128)(2,1)}, bf16[768,384]{1,0:T(8,128)(2,1)}, bf16[384,768]{1,0:T(8,128)(2,1)}) async-done(((bf16[768,384]{0,1:T(8,128)(2,1)}, bf16[768,384]{1,0:T(8,128)(2,1)}, bf16[384,768]{1,0:T(8,128)(2,1)}), (bf16[768,384]{0,1:T(8,128)(2,1)}, bf16[768,384]{1,0:T(8,128)(2,1)}, bf16[384,768]{1,0:T(8,128)(2,1)})) %all-reduce.11.cloned.1.call-update) | async-done | bytes 1769488 | tf_op jit(solution)/shard_map/psum | solution.py:236
  (247 shorter events, 147.0 us)
Async XLA Ops:
  7.2 44.0 %copy-start.22 = (bf16[1024,768]{1,0:T(8,128)(2,1)S(1)}, bf16[1024,768]{1,0:T(8,128)(2,1)}, u32[]{:S(2)}) copy-start(bf16[1024,768]{1,0:T(8,128)(2,1)} %param.12) | copy-start | bytes 4718596
  7.2 57.1 %all-gather.4.cloned.1.call-start = ((), (), s32[]{:S(2)}) async-start(), calls=%async_computation.3 | async-start | bytes 5308416 | tf_op jit(solution)/shard_map/all_gather | solution.py:96
  7.9 118.2 %all-gather.6.cloned.1.call-start = ((), (), s32[]{:S(2)}) async-start(), calls=%async_computation.4 | async-start | bytes 5308416 | tf_op jit(solution)/shard_map/all_gather | solution.py:100
  8.7 158.9 %all-gather.8.cloned.1.call-start = ((), (), s32[]{:S(2)}) async-start(), calls=%async_computation.5 | async-start | bytes 5308416 | tf_op jit(solution)/shard_map/all_gather | solution.py:101
  9.4 358.5 %reduce-scatter.6.cloned.1.call-start = ((), (), s32[]{:S(2)}) async-start(), calls=%async_computation.7 | async-start | bytes 10616832 | tf_op jit(solution)/shard_map/reduce_scatter | solution.py:183
  125.6 38.8 %copy-start.14 = (f32[1024,768]{0,1:T(8,128)}, f32[1024,768]{0,1:T(8,128)S(1)}, u32[]{:S(2)}) copy-start(f32[1024,768]{0,1:T(8,128)S(1)} %get-tuple-element.245) | copy-start | bytes 9437188
  126.1 41.5 %copy-start.45 = (f32[1,4,2,128]{3,1,2,0:T(4,128)S(1)}, f32[1,4,2,128]{3,1,2,0:T(4,128)}, u32[]{:S(2)}) copy-start(f32[1,4,2,128]{3,1,2,0:T(4,128)} %copy.100) | copy-start | bytes 12292
  126.1 41.5 %copy-start.46 = (f32[768]{0:T(1024)S(1)}, f32[768]{0:T(1024)}, u32[]{:S(2)}) copy-start(f32[768]{0:T(1024)} %get-tuple-element.257) | copy-start | bytes 9220
  167.6 18.9 %copy-start.49 = (f32[1024,3072]{1,0:T(8,128)S(1)}, f32[1024,3072]{1,0:T(8,128)}, u32[]{:S(2)}) copy-start(f32[1024,3072]{1,0:T(8,128)} %get-tuple-element.269) | copy-start | bytes 37748740
  186.5 12.3 %copy-start.27 = (bf16[1024,768]{0,1:T(8,128)(2,1)}, bf16[1024,768]{0,1:T(8,128)(2,1)S(1)}, u32[]{:S(2)}) copy-start(bf16[1024,768]{0,1:T(8,128)(2,1)S(1)} %get-tuple-element.239) | copy-start | bytes 4718596
  186.5 14.9 %copy-start.15 = (f32[1024,768]{0,1:T(8,128)S(1)}, f32[1024,768]{0,1:T(8,128)}, u32[]{:S(2)}) copy-start(f32[1024,768]{0,1:T(8,128)} %copy-done.14) | copy-start | bytes 9437188
  209.2 201.6 %reduce-scatter.4.cloned.1.call-start = ((), (), s32[]{:S(2)}) async-start(), calls=%async_computation.6 | async-start | bytes 10616832 | tf_op jit(solution)/shard_map/reduce_scatter | solution.py:232
  209.9 12.5 %copy-start.16 = (f32[1024,768]{0,1:T(8,128)S(1)}, f32[1024,768]{0,1:T(8,128)}, u32[]{:S(2)}) copy-start(f32[1024,768]{0,1:T(8,128)} %copy-done.14) | copy-start | bytes 9437188
  265.3 7.4 %copy-start.8 = (bf16[2,512,12,64]{1,3,2,0:T(8,128)(2,1)}, bf16[2,512,12,64]{1,3,2,0:T(8,128)(2,1)S(1)}, u32[]{:S(2)}) copy-start(bf16[2,512,12,64]{1,3,2,0:T(8,128)(2,1)S(1)} %fusion.157) | copy-start | bytes 4718596 | tf_op jit(solution)/shard_map/while
  311.6 199.2 %reduce-scatter.8.cloned.1.call-start = ((), (), s32[]{:S(2)}) async-start(), calls=%async_computation.8 | async-start | bytes 10616832 | tf_op jit(solution)/shard_map/reduce_scatter | solution.py:184
  321.7 256.0 %all-reduce.11.cloned.1.call-start = ((), (), s32[]{:S(2)}) async-start(), calls=%async_computation.9 | async-start | bytes 3538944 | tf_op jit(solution)/shard_map/psum | solution.py:236
  367.8 145.2 %copy-start.37 = (f32[768]{0:T(1024)S(1)}, f32[768]{0:T(1024)}, u32[]{:S(2)}) copy-start(f32[768]{0:T(1024)} %get-tuple-element.240) | copy-start | bytes 9220
  367.8 145.3 %copy-start.44 = (f32[768]{0:T(1024)S(1)}, f32[768]{0:T(1024)}, u32[]{:S(2)}) copy-start(f32[768]{0:T(1024)} %get-tuple-element.180) | copy-start | bytes 9220
  367.8 145.3 %copy-start.43 = (f32[768]{0:T(1024)S(1)}, f32[768]{0:T(1024)}, u32[]{:S(2)}) copy-start(f32[768]{0:T(1024)} %get-tuple-element.185) | copy-start | bytes 9220
  367.8 145.3 %copy-start.35 = (f32[768]{0:T(1024)S(1)}, f32[768]{0:T(1024)}, u32[]{:S(2)}) copy-start(f32[768]{0:T(1024)} %get-tuple-element.238) | copy-start | bytes 9220
  367.8 145.3 %copy-start.40 = (f32[768]{0:T(1024)S(1)}, f32[768]{0:T(1024)}, u32[]{:S(2)}) copy-start(f32[768]{0:T(1024)} %get-tuple-element.182) | copy-start | bytes 9220
  367.9 145.3 %copy-start.41 = (f32[768]{0:T(1024)S(1)}, f32[768]{0:T(1024)}, u32[]{:S(2)}) copy-start(f32[768]{0:T(1024)} %get-tuple-element.187) | copy-start | bytes 9220
  367.9 145.3 %copy-start.42 = (f32[3072]{0:T(1024)S(1)}, f32[3072]{0:T(1024)}, u32[]{:S(2)}) copy-start(f32[3072]{0:T(1024)} %get-tuple-element.271) | copy-start | bytes 36868
  370.1 180.8 %copy-start.19 = (bf16[1024,768]{0,1:T(8,128)(2,1)S(1)}, bf16[1024,768]{0,1:T(8,128)(2,1)}, u32[]{:S(2)}) copy-start(bf16[1024,768]{0,1:T(8,128)(2,1)} %get-tuple-element.252) | copy-start | bytes 4718596
  (44 other events, 137.2 us)
Sparse Core Ops, SparseCore 0:
  9.6 54.6 all-gather.3
  65.9 50.1 all-gather.5
  117.7 49.8 all-gather.7
  209.3 98.1 reduce-scatter.5
  311.8 98.9 reduce-scatter.3
  412.9 97.8 reduce-scatter.7
  514.9 62.7 all-reduce.10
where the time goes:
time: 598 us; the launch traced here: 590 us
  waiting for transfers between devices  170 us (28%)
  matrix products  168 us (28%)
  blocking collectives  109 us (18%)
  local copies, waits for them, and re-layouts  69.8 us (12%)
  other arithmetic  53.7 us (9%)
  between operations  18.8 us (3%)
    reduce_scatter x1, waiting for transfers between devices, per_device(): lax.psum_scatter(contract_grad, 'fsdp', scatter_dimension=0, tiled=True)  97.9 us
    unnamed x2, blocking collectives  58.6 us
    reduce_scatter x1, waiting for transfers between devices, per_device(): lax.psum_scatter(attention_grad, 'fsdp', scatter_dimension=1, tiled=True)  40.7 us
    psum x1, blocking collectives, per_device(): square_sums, count_total = lax.psum((squares, count_sum), ('dp', 'fsdp'))  40.2 us
    dot_general x1, matrix products, per_device(): jnp.dot(hidden_low, expand_whole, preferred_element_type=jnp.float32)  38.3 us
    unnamed x109, local copies, waits for them, and re-layouts  24.2 us
    dot_general x2, matrix products, attend_back(): jnp.einsum('qhd,khd->hqk', context_grad, value_rows, preferred_element_ty...  14.7 us
    convert_element_type x2, other arithmetic, attend_back(): score_grad = (softmax_wide * (weight_grad - row_total)).astype(jnp.bfloat16)  14.6 us
  transfers between devices with their start and end apart: 7, of which 5 were waited for; matrix products, arithmetic and copies ran while one was open for 40% of the time, Pallas kernels for 0%

commit v1 on v0

--- a/solution.py
+++ b/solution.py
@@ -8,6 +8,12 @@
 FF = 3072
 EPSILON = 1e-12
 NEGATIVE = -1000000000.0
+
+
+def limits_push(obj, chip_axis):
+    x_new = jax.lax.all_gather(obj, axis_name=chip_axis)
+    val2 = jnp.sum(x_new, axis=0)
+    return val2
 
 
 def norm_forward(residual, scale_gain, shift_bias):
@@ -233,7 +239,7 @@
         lax.psum_scatter(attvec_grad, "fsdp", scatter_dimension=0, tiled=True),
     )
     finished = (
-        lax.psum(attn_shards[0].astype(jnp.bfloat16), "dp").astype(jnp.float32),
+        limits_push(attn_shards[0].astype(jnp.bfloat16), chip_axis="dp").astype(jnp.float32),
         lax.psum(attn_shards[1].astype(jnp.bfloat16), "dp").astype(jnp.float32),
         lax.psum(feed_shards[0].astype(jnp.bfloat16), "dp").astype(jnp.float32),
         lax.psum(feed_shards[1].astype(jnp.bfloat16), "dp").astype(jnp.float32),

time: 598 us -> 638 us (1.067)
  waiting for transfers between devices: 170 us -> 194 us
  matrix products: 168 us -> 180 us
    reduce_scatter x1, waiting for transfers between devices: 40.7 us -> 97.8 us  [per_device(): lax.psum_scatter(attention_grad, 'fsdp', scatter_dimension=1, tiled=True)]
    reduce_scatter x1, waiting for transfers between devices: 97.9 us -> 82.7 us  [per_device(): lax.psum_scatter(contract_grad, 'fsdp', scatter_dimension=0, tiled=True)]
    psum x1, waiting for transfers between devices: 14.3 us -> 0.01 us  [per_device(): lax.psum(feed_shards[0].astype(jnp.bfloat16), 'dp').astype(jnp.float32)]
    dot_general x1, matrix products: 38.3 us -> 49.3 us  [per_device(): jnp.dot(hidden_low, expand_whole, preferred_element_type=jnp.float32)]
    unnamed x109 -> x111, local copies, waits for them, and re-layouts: 24.2 us -> 23.7 us
  transfers between devices with their start and end apart: 7 -> 8, of which waited for: 5 -> 3; matrix products, arithmetic and copies ran while one was open for 40% -> 40% of each run, Pallas kernels for 0% -> 0%
where the time goes in v1:
time: 638 us; the launch traced here: 631 us
  waiting for transfers between devices  194 us (30%)
  matrix products  180 us (28%)
  blocking collectives  108 us (17%)
  local copies, waits for them, and re-layouts  71.5 us (11%)
  other arithmetic  57.5 us (9%)
  between operations  19.2 us (3%)
    reduce_scatter x1, waiting for transfers between devices, per_device(): lax.psum_scatter(attention_grad, 'fsdp', scatter_dimension=1, tiled=True)  97.8 us
    reduce_scatter x1, waiting for transfers between devices, per_device(): lax.psum_scatter(contract_grad, 'fsdp', scatter_dimension=0, tiled=True)  82.7 us
    unnamed x2, blocking collectives  60.2 us
    dot_general x1, matrix products, per_device(): jnp.dot(hidden_low, expand_whole, preferred_element_type=jnp.float32)  49.3 us
    psum x1, blocking collectives, per_device(): square_sums, count_total = lax.psum((squares, count_sum), ('dp', 'fsdp'))  38.1 us
    unnamed x111, local copies, waits for them, and re-layouts  23.7 us
    convert_element_type x2, other arithmetic, attend_back(): score_grad = (softmax_wide * (weight_grad - row_total)).astype(jnp.bfloat16)  14.8 us
    dot_general x2, matrix products, attend_back(): jnp.einsum('qhd,khd->hqk', context_grad, value_rows, preferred_element_ty...  14.6 us
  transfers between devices with their start and end apart: 8, of which 3 were waited for; matrix products, arithmetic and copies ran while one was open for 40% of the time, Pallas kernels for 0%

profile of v1, /device:TPU:0, one launch (start us, length us, event | category | flops | bytes accessed | tf_op | source)
XLA Modules:
  0.0 630.5 jit_solution(10529228960058733106)
XLA Ops:
  13.9 32.2 %all-reduce.6 = (bf16[3840]{0:T(1024)(128)(2,1)S(1)}, bf16[5376]{0:T(1024)(128)(2,1)S(1)}) all-reduce(bf16[3840]{0:T(1024)(128)(2,1)S(1)} %dynamic-update-slice, bf16[5376]{0:T(1024)(128)(2,1)S(1)} %dynamic-update-slice.1), channel_id=1, replica_groups=mesh['dp'=4,'fsdp'=8] {'fsdp'}, use_global_device_ids=true, to_apply=%add | all-reduce | flops 9216 | bytes 36864
  52.9 11.4 %all-gather.6.cloned.1.call-done = bf16[768,3072]{1,0:T(8,128)(2,1)} async-done(((bf16[768,384]{1,0:T(8,128)(2,1)}), bf16[768,3072]{1,0:T(8,128)(2,1)}) %all-gather.6.cloned.1.call-update) | async-done | bytes 4718608 | tf_op jit(solution)/shard_map/all_gather | solution.py:102
  64.3 5.8 fusion.87
  94.2 19.3 %while.26 = (s32[]{:T(128)}, bf16[2,512,12,64]{1,3,2,0:T(8,128)(2,1)}, f32[2,12,512]{2,1,0:T(8,128)S(1)}, bf16[2,512,12,64]{1,3,2,0:T(8,128)(2,1)}, pred[2,512]{...) while((s32[]{:T(128)}, ...), condition=%wide.region_3.4_spmd, body=%wide.region_0.3_spmd.sunk | while | flops 840296448 | bytes 47428216 | solution.py:133
  118.2 5.1 fusion.105
  123.8 49.3 %fusion.59 = (bf16[1024,3072]{1,0:T(8,128)(2,1)}, f32[1024,3072]{1,0:T(8,128)}) fusion(f32[3072]{0:T(1024)S(1)} %slice.77, bf16[768,3072]{1,0:T(8,128)(2,1)} %all-gather.8.cloned.1.call-done, f32[1024,768]{0,1:T(8,128)S(1)} %get-tuple-element.244, f32[768]{0:T(1024)S(1)} %get-tuple-element.258, f32[768]{0:T(1024)S(1)} %get-tuple-element.257, ...), kind=kOutput, calls=%fused_computation.67 | convolution fusion | flops 5043388416 | bytes 26765312 | tf_op jit(solution)/shard_map/dot_general | solution.py:143
  173.2 12.2 %fusion.80 = (f32[]{:T(128)}, f32[]{:T(128)}, f32[]{:T(128)}, f32[1024]{0:T(1024)S(1)}, f32[1024,768]{0,1:T(8,128)S(1)}) fusion(bf16[1024,768]{0,1:T(8,128)(2,1)} %copy.64, f32[1024]{0:T(1024)S(1)} %bitcast.167, f32[1024,768]{0,1:T(8,128)} %get-tuple-element.266, f32[768]{0:T(1024)S(1)} %get-tuple-element.259, f32[768]{0:T(1024)S(1)} %copy-done.45, ...), kind=kOutput, calls=%fused_computation.106 | convolution fusion | flops 4845992960 | bytes 22048780 | tf_op jit(solution)/shard_map/dot_general | solution.py:145
  192.1 12.3 %convert_reduce_fusion = (f32[3072]{0:T(1024)}, bf16[1024,3072]{1,0:T(8,128)(2,1)S(1)}) fusion(f32[1024,3072]{1,0:T(8,128)S(1)} %copy-done.48, f32[3072]{0:T(1024)S(1)} %slice.77, bf16[1024,768]{0,1:T(8,128)(2,1)S(1)} %get-tuple-element.238, bf16[3072,768]{1,0:T(8,128)(2,1)S(1)} %bitcast.169), kind=kOutput, calls=%fused_computation.74 | convolution fusion | flops 4872729600 | bytes 25190400 | tf_op jit(solution)/shard_map/nd,fd->nf/dot_general | solution.py:177
  206.9 7.8 %fusion.99 = f32[768,3072]{1,0:T(8,128)} fusion(bf16[1024,3072]{1,0:T(8,128)(2,1)S(1)} %get-tuple-element.271, f32[1024,768]{0,1:T(8,128)S(1)} %copy-done.13, f32[768]{0:T(1024)S(1)} %get-tuple-element.258, f32[768]{0:T(1024)S(1)} %get-tuple-element.257, f32[1024]{0:T(1024)S(1)} %add_rsqrt_fusion.1, f32[1024]{0:T(1024)S(1)} %broadcast_multiply_fusion.5), kind=kOutput, calls=%fused_computation.169 | convolution fusion | flops 4835770368 | bytes 18888704 | tf_op jit(solution)/shard_map/nd,nf->df/dot_general | solution.py:182
  214.8 10.4 %fusion.109 = f32[3072,768]{1,0:T(8,128)} fusion(bf16[1024,3072]{1,0:T(8,128)(2,1)} %get-tuple-element.267, bf16[1024,768]{0,1:T(8,128)(2,1)} %copy-done.27), kind=kOutput, calls=%fused_computation.176 | convolution fusion | flops 4831838208 | bytes 17301504 | tf_op jit(solution)/shard_map/nf,nd->fd/dot_general | solution.py:174
  225.8 12.2 %multiply_reduce_fusion.1 = (f32[768]{0:T(1024)}, f32[1024]{0:T(1024)S(1)}, f32[1024]{0:T(1024)S(1)}, f32[768]{0:T(1024)}, f32[1024,768]{0,1:T(8,128)S(1)}) fusion(f32[1024,768]{0,1:T(8,128)} %copy-done.12, f32[1024]{0:T(1024)S(1)} %add_rsqrt_fusion.1, f32[1024]{0:T(1024)S(1)} %broadcast_multiply_fusion.5, f32[768]{0:T(1024)S(1)} %copy-done.35, ...), kind=kOutput, calls=%fused_computation.115 | convolution fusion | flops 4845989888 | bytes 22065152 | tf_op jit(solution)/shard_map/nf,df->nd/dot_general | solution.py:193
  251.7 50.1 %while.27 = (s32[]{:T(128)}, bf16[2,512,12,64]{1,3,2,0:T(8,128)(2,1)}, bf16[2,512,12,64]{1,3,2,0:T(8,128)(2,1)}, bf16[2,512,12,64]{1,3,2,0:T(8,128)(2,1)}, bf16[...) while((s32[]{:T(128)}, ...), condition=%wide.region_14.15_spmd, body=%wide.region_12.14_spmd.sunk | while | flops 2062411776 | bytes 140181296 | solution.py:210
  253.9 7.3 %multiply_reduce_fusion.7 = (f32[12,512]{1,0:T(8,128)S(1)}, f32[12,512,512]{1,2,0:T(8,128)}) fusion(f32[12,512,512]{1,2,0:T(8,128)S(1)} %fusion.154, f32[12,512]{1,0:T(8,128)S(1)} %dynamic-slice_bitcast_fusion.2, pred[512]{0:T(512)(128)(4,1)S(1)} %dynamic-slice_reduce_fusion.5, bf16[2,512,12,64]{1,3,2,0:T(8,128)(2,1)S(1)} %copy-done.5, ...), kind=kOutput, calls=%fused_computation.24.clone.1 | convolution fusion | flops 418375680 | bytes 26797568 | tf_op jit(solution)/shard_map/while/body/eval_jaxpr/qhd,khd->hqk/dot_general | solution.py:66
  261.2 7.4 %multiply_convert_fusion.4 = bf16[12,512,512]{1,2,0:T(8,128)(2,1)S(1)} fusion(f32[12,512,512]{1,2,0:T(8,128)} %get-tuple-element.388, f32[12,512,512]{1,2,0:T(8,128)S(1)} %fusion.154, f32[12,512]{1,0:T(8,128)S(1)} %get-tuple-element.389, f32[12,512]{1,0:T(8,128)S(1)} %dynamic-slice_bitcast_fusion.2, pred[512]{0:T(512)(128)(4,1)S(1)} %dynamic-slice_reduce_fusion.5), kind=kLoop, calls=%fused_computation.23.clone.1 | loop fusion | flops 18874368 | bytes 31506944 | tf_op jit(solution)/shard_map/while/body/eval_jaxpr/convert_element_type | solution.py:70
  278.7 7.3 %multiply_reduce_fusion.7 = (f32[12,512]{1,0:T(8,128)S(1)}, f32[12,512,512]{1,2,0:T(8,128)}) fusion(f32[12,512,512]{1,2,0:T(8,128)S(1)} %fusion.154, f32[12,512]{1,0:T(8,128)S(1)} %dynamic-slice_bitcast_fusion.2, pred[512]{0:T(512)(128)(4,1)S(1)} %dynamic-slice_reduce_fusion.5, bf16[2,512,12,64]{1,3,2,0:T(8,128)(2,1)S(1)} %copy-done.5, ...), kind=kOutput, calls=%fused_computation.24.clone.1 | convolution fusion | flops 418375680 | bytes 26797568 | tf_op jit(solution)/shard_map/while/body/eval_jaxpr/qhd,khd->hqk/dot_general | solution.py:66
  286.0 7.4 %multiply_convert_fusion.4 = bf16[12,512,512]{1,2,0:T(8,128)(2,1)S(1)} fusion(f32[12,512,512]{1,2,0:T(8,128)} %get-tuple-element.388, f32[12,512,512]{1,2,0:T(8,128)S(1)} %fusion.154, f32[12,512]{1,0:T(8,128)S(1)} %get-tuple-element.389, f32[12,512]{1,0:T(8,128)S(1)} %dynamic-slice_bitcast_fusion.2, pred[512]{0:T(512)(128)(4,1)S(1)} %dynamic-slice_reduce_fusion.5), kind=kLoop, calls=%fused_computation.23.clone.1 | loop fusion | flops 18874368 | bytes 31506944 | tf_op jit(solution)/shard_map/while/body/eval_jaxpr/convert_element_type | solution.py:70
  314.6 6.0 convolution_bitcast_fusion
  320.6 7.3 %pad_maximum_fusion = f32[768,3072]{0,1:T(8,128)} fusion(f32[768,768]{0,1:T(8,128)S(1)} %fusion.96, f32[768,2304]{0,1:T(8,128)} %convolution_bitcast_fusion), kind=kLoop, calls=%fused_computation.90 | loop fusion | flops 2359296 | bytes 18874368 | tf_op jit(solution)/shard_map/concatenate | solution.py:233
  330.3 82.7 %reduce-scatter.8.cloned.1.call-done = f32[384,768]{1,0:T(8,128)} async-done(((f32[3072,768]{1,0:T(8,128)}), f32[384,768]{1,0:T(8,128)}) %reduce-scatter.8.cloned.1.call-update) | async-done | bytes 1179664 | tf_op jit(solution)/shard_map/reduce_scatter | solution.py:190
  415.3 97.8 %reduce-scatter.4.cloned.1.call-done = f32[768,384]{0,1:T(8,128)} async-done(((f32[768,3072]{0,1:T(8,128)}), f32[768,384]{0,1:T(8,128)}) %reduce-scatter.4.cloned.1.call-update) | async-done | bytes 1179664 | tf_op jit(solution)/shard_map/reduce_scatter | solution.py:238
  519.8 38.1 %all-reduce.4 = (f32[3]{0:T(128)S(1)}, f32[]{:T(128)}) all-reduce(f32[3]{0:T(128)S(1)} %pad_maximum_fusion.2, f32[]{:T(128)S(6)} %convert_element_type.178), channel_id=1, replica_groups=mesh['dp'=4,'fsdp'=8] {'dp','fsdp'}, use_global_device_ids=true, to_apply=%region_37.38 | all-reduce | flops 4 | bytes 32 | tf_op jit(solution)/shard_map/psum | solution.py:156
  558.7 28.0 %all-reduce.5 = (bf16[3840]{0:T(1024)(128)(2,1)S(1)}, bf16[5376]{0:T(1024)(128)(2,1)S(1)}) all-reduce(f32[3840]{0:T(1024)S(1)} %constant_dynamic-update-slice_fusion.6, f32[5376]{0:T(1024)S(1)} %pad_maximum_fusion.1), channel_id=4, replica_groups=mesh['dp'=4,'fsdp'=8] {'fsdp'}, use_global_device_ids=true, to_apply=%region_22.23.clone | all-reduce | flops 9216 | bytes 55296
  586.8 9.3 %all-reduce.7 = (bf16[480]{0:T(512)(128)(2,1)S(1)}, bf16[672]{0:T(1024)(128)(2,1)S(1)}) all-reduce(bf16[480]{0:T(512)(128)(2,1)S(1)} %dynamic-slice.9, bf16[672]{0:T(1024)(128)(2,1)S(1)} %dynamic-slice.8), channel_id=1, replica_groups=mesh['dp'=4,'fsdp'=8] {'dp'}, use_global_device_ids=true, to_apply=%region_23.24 | all-reduce | flops 1152 | bytes 4608 | tf_op jit(solution)/shard_map/psum | solution.py:243
  597.3 8.3 %add_convert_fusion = bf16[1024,768]{0,1:T(8,128)(2,1)S(1)} fusion(f32[1024,768]{0,1:T(8,128)} %copy-done.19, bf16[1024,2304]{0,1:T(8,128)(2,1)} %copy-done.28, bf16[768,3072]{1,0:T(8,128)(2,1)} %all-gather.6.cloned.1.call-done), kind=kOutput, calls=%fused_computation.119 | convolution fusion | flops 3625451520 | bytes 12976128 | tf_op jit(solution)/shard_map/ne,de->nd/dot_general | solution.py:227
  (246 shorter events, 144.8 us)
Async XLA Ops:
  7.2 44.1 %copy-start.21 = (bf16[1024,768]{1,0:T(8,128)(2,1)S(1)}, bf16[1024,768]{1,0:T(8,128)(2,1)}, u32[]{:S(2)}) copy-start(bf16[1024,768]{1,0:T(8,128)(2,1)} %param.19) | copy-start | bytes 4718596
  7.2 57.1 %all-gather.6.cloned.1.call-start = ((), (), s32[]{:S(2)}) async-start(), calls=%async_computation.3 | async-start | bytes 5308416 | tf_op jit(solution)/shard_map/all_gather | solution.py:102
  7.9 115.8 %all-gather.8.cloned.1.call-start = ((), (), s32[]{:S(2)}) async-start(), calls=%async_computation.4 | async-start | bytes 5308416 | tf_op jit(solution)/shard_map/all_gather | solution.py:106
  8.7 164.5 %all-gather.10.cloned.1.call-start = ((), (), s32[]{:S(2)}) async-start(), calls=%async_computation.5 | async-start | bytes 5308416 | tf_op jit(solution)/shard_map/all_gather | solution.py:107
  9.4 318.6 %reduce-scatter.6.cloned.1.call-start = ((), (), s32[]{:S(2)}) async-start(), calls=%async_computation.7 | async-start | bytes 10616832 | tf_op jit(solution)/shard_map/reduce_scatter | solution.py:189
  48.0 16.3 %copy-start.22 = (bf16[1024,768]{1,0:T(8,128)(2,1)S(1)}, bf16[1024,768]{1,0:T(8,128)(2,1)}, u32[]{:S(2)}) copy-start(bf16[1024,768]{1,0:T(8,128)(2,1)} %param.12) | copy-start | bytes 4718596
  123.3 49.8 %copy-start.12 = (f32[1024,768]{0,1:T(8,128)}, f32[1024,768]{0,1:T(8,128)S(1)}, u32[]{:S(2)}) copy-start(f32[1024,768]{0,1:T(8,128)S(1)} %get-tuple-element.244) | copy-start | bytes 9437188
  123.8 49.4 %copy-start.44 = (f32[1,4,2,128]{3,1,2,0:T(4,128)S(1)}, f32[1,4,2,128]{3,1,2,0:T(4,128)}, u32[]{:S(2)}) copy-start(f32[1,4,2,128]{3,1,2,0:T(4,128)} %copy.98) | copy-start | bytes 12292
  123.8 49.4 %copy-start.45 = (f32[768]{0:T(1024)S(1)}, f32[768]{0:T(1024)}, u32[]{:S(2)}) copy-start(f32[768]{0:T(1024)} %get-tuple-element.256) | copy-start | bytes 9220
  173.2 18.9 %copy-start.48 = (f32[1024,3072]{1,0:T(8,128)S(1)}, f32[1024,3072]{1,0:T(8,128)}, u32[]{:S(2)}) copy-start(f32[1024,3072]{1,0:T(8,128)} %get-tuple-element.268) | copy-start | bytes 37748740
  192.1 14.9 %copy-start.13 = (f32[1024,768]{0,1:T(8,128)S(1)}, f32[1024,768]{0,1:T(8,128)}, u32[]{:S(2)}) copy-start(f32[1024,768]{0,1:T(8,128)} %copy-done.12) | copy-start | bytes 9437188
  214.7 198.2 %reduce-scatter.8.cloned.1.call-start = ((), (), s32[]{:S(2)}) async-start(), calls=%async_computation.8 | async-start | bytes 10616832 | tf_op jit(solution)/shard_map/reduce_scatter | solution.py:190
  225.2 287.9 %reduce-scatter.4.cloned.1.call-start = ((), (), s32[]{:S(2)}) async-start(), calls=%async_computation.6 | async-start | bytes 10616832 | tf_op jit(solution)/shard_map/reduce_scatter | solution.py:238
  327.9 187.3 %copy-start.46 = (s32[2]{0:T(128)S(1)}, s32[2]{0:T(128)}, u32[]{:S(2)}) copy-start(s32[2]{0:T(128)} %param.18) | copy-start | bytes 28
  327.9 229.9 %copy-start.9 = (bf16[2,512,12,64]{1,3,2,0:T(8,128)(2,1)S(1)}, bf16[2,512,12,64]{1,3,2,0:T(8,128)(2,1)}, u32[]{:S(2)}) copy-start(bf16[2,512,12,64]{1,3,2,0:T(8,128)(2,1)} %get-tuple-element.102) | copy-start | bytes 4718596
  327.9 282.0 %all-reduce.11.cloned.1.call-start = ((), (), s32[]{:S(2)}) async-start(), calls=%async_computation.10 | async-start | bytes 2359296 | tf_op jit(solution)/shard_map/psum | solution.py:244
  415.1 143.4 %copy-start.36 = (f32[768]{0:T(1024)S(1)}, f32[768]{0:T(1024)}, u32[]{:S(2)}) copy-start(f32[768]{0:T(1024)} %get-tuple-element.239) | copy-start | bytes 9220
  415.1 143.4 %copy-start.43 = (f32[768]{0:T(1024)S(1)}, f32[768]{0:T(1024)}, u32[]{:S(2)}) copy-start(f32[768]{0:T(1024)} %get-tuple-element.180) | copy-start | bytes 9220
  415.1 143.4 %copy-start.42 = (f32[768]{0:T(1024)S(1)}, f32[768]{0:T(1024)}, u32[]{:S(2)}) copy-start(f32[768]{0:T(1024)} %get-tuple-element.185) | copy-start | bytes 9220
  415.1 143.5 %copy-start.34 = (f32[768]{0:T(1024)S(1)}, f32[768]{0:T(1024)}, u32[]{:S(2)}) copy-start(f32[768]{0:T(1024)} %get-tuple-element.237) | copy-start | bytes 9220
  415.2 143.5 %copy-start.39 = (f32[768]{0:T(1024)S(1)}, f32[768]{0:T(1024)}, u32[]{:S(2)}) copy-start(f32[768]{0:T(1024)} %get-tuple-element.182) | copy-start | bytes 9220
  415.2 143.5 %copy-start.40 = (f32[768]{0:T(1024)S(1)}, f32[768]{0:T(1024)}, u32[]{:S(2)}) copy-start(f32[768]{0:T(1024)} %get-tuple-element.187) | copy-start | bytes 9220
  415.2 143.5 %copy-start.41 = (f32[3072]{0:T(1024)S(1)}, f32[3072]{0:T(1024)}, u32[]{:S(2)}) copy-start(f32[3072]{0:T(1024)} %get-tuple-element.270) | copy-start | bytes 36868
  415.2 199.1 %all-gather.12.cloned.1.call-start = ((), (), s32[]{:S(2)}) async-start(), calls=%async_computation.9 | async-start | bytes 2949120 | tf_op jit(solution)/shard_map/all_gather | solution.py:14
  (42 other events, 144.2 us)
Sparse Core Ops, SparseCore 0:
  9.6 54.6 all-gather.5
  65.9 50.1 all-gather.7
  117.7 49.8 all-gather.9
  214.9 97.9 reduce-scatter.5
  315.1 97.8 reduce-scatter.7
  415.2 97.8 reduce-scatter.3
  516.8 53.6 all-reduce.10
  572.9 37.4 all-gather.11
